TPU v7x, 32 devices: a whole 2x2x4 slice. The times are simulated.
32 devices in a mesh: section: 4 (over y, core), expert: 8 (over z, x).
Axes of the slice: x: 2, y: 2, z: 4, core: 2. Of those that a mesh axis runs over, the one named last changes fastest.
Arguments:
- activations: bfloat16 [4, 256, 4096], P('section', 'expert'), may hold values from -6 to 6
- norm_gain: float32 [4, 4096], P('section'), may hold values from 0.25 to 1.75
- in_proj: bfloat16 [4, 4096, 40960], P('section', None, 'expert'), may hold values from -0.09375 to 0.09375
- out_proj: bfloat16 [4, 40960, 4096], P('section', 'expert'), may hold values from -0.078125 to 0.078125
- expert_ids: int32 [4, 256, 1], P('section', 'expert'), may hold values from 0 to 7; in each aligned block of 32 rows (0 to 31, 32 to 63, ..., all dimensions but the last counted through in order) at most 8 rows name the same one
Outputs:
- passed: bfloat16 [4, 256, 4096], P('section', 'expert')
Inputs may be any that keep to these rules, and one draw needn't show every extreme that they name: `expert_ids`: within the 32 rows of one device (aligned blocks of 32 rows along the token dimension of each layer), no expert is named by more than 8 rows.
All inputs are finite; a program needn't handle non-finite values.
Results may differ from a plain program's by a relative error of at most 0.0047.
Values may be sent and summed in bfloat16 or wider, within the bound.
A program may use at most 128 MiB of HBM per device.

v0:
```python
import functools

import jax
import jax.numpy as jnp
from jax import lax
from jax.experimental import pallas as pl
from jax.experimental.pallas import tpu as pltpu
from jax.sharding import PartitionSpec as P

EXPERTS = 8
SLOTS = 5
MESH = pl.DeviceIdType.MESH
F32, BF16 = jnp.float32, jnp.bfloat16

epsilon = 1e-06


def divisor(size, most):
    return max(k for k in range(128, most + 1, 128) if size % k == 0)


def placement(routed, ranks, capacity, groups, count):
    row = lax.broadcasted_iota(jnp.int32, (count * capacity, routed.shape[1]), 0)
    owner = row // (capacity * groups)
    return jnp.where((owner == routed) & (row % capacity == ranks), 1.0, 0.0).astype(F32)


def kernel(
    sections, n, capacity, act_hbm, gain_hbm, ids_hbm, first_hbm, second_hbm, out,
    act, gain, ids, first, second, normed, packed, received, total, hidden, outgoing, returned,
    where_to, residual, where_from,
    small_sem, first_sem, second_sem, pass_send, pass_recv, send_sem, recv_sem, back_send, back_recv,
):
    section, me = lax.axis_index("section"), lax.axis_index("expert")
    following = lax.rem(section + 1, sections)
    groups = n // EXPERTS
    tokens, width = act.shape
    ff = hidden.shape[1]
    chunks, depth = packed.shape[0], packed.shape[3]
    tiles, columns = outgoing.shape[0], outgoing.shape[3]
    loads = chunks + tiles

    def load(step, is_first):
        if is_first:
            rows = pl.ds(pl.multiple_of(step * depth, depth), depth)
            slot = lax.rem(step, SLOTS)
            return pltpu.make_async_copy(first_hbm.at[0, rows, :], first.at[slot], first_sem.at[slot])
        cols = pl.ds(pl.multiple_of(step * columns, columns), columns)
        slot = lax.rem(step, SLOTS)
        return pltpu.make_async_copy(second_hbm.at[0, :, cols], second.at[slot], second_sem.at[slot])

    smalls = [
        pltpu.make_async_copy(act_hbm.at[0], act, small_sem.at[0]),
        pltpu.make_async_copy(gain_hbm, gain, small_sem.at[1]),
        pltpu.make_async_copy(ids_hbm, ids, small_sem.at[2]),
    ]
    barrier = pltpu.get_barrier_semaphore()
    shifts = (0, sections - 1)
    for shift in shifts:
        peer_section = lax.rem(section + shift, sections)

        def greet(i, carry):
            peer = lax.rem(me + i, n)
            pl.semaphore_signal(barrier, inc=1, device_id=(peer_section, peer), device_id_type=MESH)
            return carry

        lax.fori_loop(1 if shift == 0 else 0, n, greet, 0)

    for copy in smalls:
        copy.start()
    for step in range(SLOTS):
        load(jnp.int32(step), True).start()

    for copy in smalls:
        copy.wait()
    floats = act[...].astype(F32)
    scale = lax.rsqrt(jnp.mean(floats * floats, axis=-1, keepdims=True) + epsilon)
    normed[...] = (floats * scale * gain[...]).astype(BF16)
    routed = ids[...]
    expert = lax.broadcasted_iota(jnp.int32, (EXPERTS, tokens), 0)
    onehot = jnp.where(expert == routed, 1.0, 0.0).astype(F32)
    earlier = lax.broadcasted_iota(jnp.int32, (tokens, tokens), 0) < lax.broadcasted_iota(
        jnp.int32, (tokens, tokens), 1
    )
    before = jnp.dot(
        onehot.astype(BF16), jnp.where(earlier, 1.0, 0.0).astype(BF16), preferred_element_type=F32
    )
    ranks = jnp.sum(before * onehot, axis=0, keepdims=True).astype(jnp.int32)
    placing = placement(routed, ranks, capacity, 1, EXPERTS).astype(BF16)
    back = placement(routed, ranks, capacity, groups, where_to.shape[1] // capacity)
    where_to[...] = back.T.astype(BF16)

    pl.semaphore_wait(barrier, len(shifts) * n - 1)

    half = n // 2
    for c in range(chunks):
        block = jnp.dot(placing, normed[:, c * depth:(c + 1) * depth], preferred_element_type=F32)
        packed[c] = block.astype(BF16).reshape(EXPERTS, capacity, depth)

        def dispatch(i, carry):
            step = (i + 1) // 2
            peer = lax.rem(me + half + jnp.where(lax.rem(i, 2) == 0, step, n - step), n)
            pltpu.make_async_remote_copy(
                src_ref=packed.at[c, peer // groups],
                dst_ref=received.at[c, me],
                send_sem=send_sem.at[c],
                recv_sem=recv_sem.at[c],
                device_id=(section, peer),
                device_id_type=MESH,
            ).start()
            return carry

        lax.fori_loop(0, n - 1, dispatch, 0)
        pltpu.make_async_copy(packed.at[c, me // groups], received.at[c, me], recv_sem.at[c]).start()

    passes = [
        pltpu.make_async_remote_copy(
            src_ref=src, dst_ref=dst, send_sem=pass_send.at[k], recv_sem=pass_recv.at[k],
            device_id=(following, me), device_id_type=MESH,
        )
        for k, (src, dst) in enumerate(((act, residual), (where_to, where_from)))
    ]
    for copy in passes:
        copy.start()

    sub = divisor(ff, 5120)

    def multiply(c, kind):
        load(c, True).wait()
        pltpu.make_async_copy(received.at[c], received.at[c], recv_sem.at[c]).wait()
        slot = lax.rem(c, SLOTS)
        rows = received[c].reshape(n * capacity, depth)

        def part(j, carry):
            cols = pl.ds(pl.multiple_of(j * sub, sub), sub)
            value = jnp.dot(rows, first[slot, :, cols], preferred_element_type=F32)
            if kind != "start":
                value = value + total[:, cols]
            if kind == "end":
                hidden[:, cols] = jax.nn.gelu(value, approximate=True).astype(BF16)
            else:
                total[:, cols] = value
            return carry

        lax.fori_loop(0, ff // sub, part, 0)

    def more(step):
        @pl.when(step < chunks)
        def _():
            load(step, True).start()

        @pl.when((step >= chunks) & (step < loads))
        def _():
            load(step - chunks, False).start()

    multiply(jnp.int32(0), "start")
    more(jnp.int32(SLOTS))

    def middle(c, carry):
        multiply(c, "middle")
        more(c + SLOTS)
        return carry

    lax.fori_loop(1, chunks - 1, middle, 0)
    multiply(jnp.int32(chunks - 1), "end")
    more(jnp.int32(chunks - 1 + SLOTS))

    sub_out = divisor(columns, 512)

    def tile(t, carry):
        load(t, False).wait()
        slot = lax.rem(t, SLOTS)
        for j in range(columns // sub_out):
            cols = slice(j * sub_out, (j + 1) * sub_out)
            piece = jnp.dot(hidden[...], second[slot, :, cols], preferred_element_type=F32)
            outgoing[t, :, :, cols] = piece.astype(BF16).reshape(n, capacity, sub_out)
        more(t + chunks + SLOTS)

        def give(i, inner):
            step = (i + 1) // 2
            peer = lax.rem(me + half + jnp.where(lax.rem(i, 2) == 0, step, n - step), n)
            pltpu.make_async_remote_copy(
                src_ref=outgoing.at[t, peer],
                dst_ref=returned.at[t, me],
                send_sem=back_send.at[t],
                recv_sem=back_recv.at[t],
                device_id=(following, peer),
                device_id_type=MESH,
            ).start()
            return inner

        lax.fori_loop(0, n, give, 0)
        return carry

    lax.fori_loop(0, tiles, tile, 0)

    for copy in passes:
        copy.wait()
    picks = where_from[:, :n * capacity]

    def combine(t, carry):
        pltpu.make_async_copy(returned.at[t], returned.at[t], back_recv.at[t]).wait()
        cols = pl.ds(pl.multiple_of(t * columns, columns), columns)
        mixed = jnp.dot(picks, returned[t].reshape(n * capacity, columns), preferred_element_type=F32)
        out[0, :, cols] = (residual[:, cols].astype(F32) + mixed).astype(BF16)
        return carry

    lax.fori_loop(0, tiles, combine, 0)

    def finish(t, carry):
        pltpu.make_async_copy(outgoing.at[t], outgoing.at[t], back_send.at[t]).wait()
        return carry

    lax.fori_loop(0, tiles, finish, 0)

    def drain(c, carry):
        done = received.at[c, pl.ds(0, n - 1)]
        pltpu.make_async_copy(done, done, send_sem.at[c]).wait()
        return carry

    lax.fori_loop(0, chunks, drain, 0)


def per_device(sections, n, activations, norm_gain, in_proj, out_proj, expert_ids):
    tokens, width = activations.shape[1:]
    ff = in_proj.shape[2]
    capacity = 2 * tokens // EXPERTS
    depth = divisor(width, 512)
    columns = divisor(width, 512)
    chunks, tiles = width // depth, width // columns
    rows = n * capacity
    lanes = max(128, rows)
    dma = pltpu.SemaphoreType.DMA
    return pl.pallas_call(
        functools.partial(kernel, sections, n, capacity),
        out_shape=pltpu.VMEM(activations.shape, activations.dtype),
        in_specs=[pl.BlockSpec(memory_space=pl.ANY)] * 5,
        out_specs=pl.BlockSpec(memory_space=pltpu.VMEM),
        scratch_shapes=[
            pltpu.VMEM((tokens, width), BF16),
            pltpu.VMEM((1, width), F32),
            pltpu.VMEM((1, tokens), jnp.int32),
            pltpu.VMEM((SLOTS, depth, ff), BF16),
            pltpu.VMEM((SLOTS, ff, columns), BF16),
            pltpu.VMEM((tokens, width), BF16),
            pltpu.VMEM((chunks, EXPERTS, capacity, depth), BF16),
            pltpu.VMEM((chunks, n, capacity, depth), BF16),
            pltpu.VMEM((rows, ff), F32),
            pltpu.VMEM((rows, ff), BF16),
            pltpu.VMEM((tiles, n, capacity, columns), BF16),
            pltpu.VMEM((tiles, n, capacity, columns), BF16),
            pltpu.VMEM((tokens, lanes), BF16),
            pltpu.VMEM((tokens, width), BF16),
            pltpu.VMEM((tokens, lanes), BF16),
            dma((3,)),
            dma((SLOTS,)),
            dma((SLOTS,)),
            dma((2,)),
            dma((2,)),
            dma((chunks,)),
            dma((chunks,)),
            dma((tiles,)),
            dma((tiles,)),
        ],
        compiler_params=pltpu.CompilerParams(
            collective_id=0, has_side_effects=True, vmem_limit_bytes=62 * 1024 * 1024
        ),
    )(activations, norm_gain, expert_ids.reshape(1, tokens), in_proj, out_proj)


def solution(mesh):
    return jax.shard_map(
        functools.partial(per_device, mesh.shape["section"], mesh.shape["expert"]),
        mesh=mesh,
        in_specs=(
            P("section", "expert", None),
            P("section", None),
            P("section", None, "expert"),
            P("section", "expert", None),
            P("section", "expert", None),
        ),
        out_specs=P("section", "expert", None),
        check_vma=False,
    )
```

profile of v0, /device:TPU:1, one launch (start us, length us, event | category | flops | bytes accessed | tf_op | source)
XLA Modules:
  0.0 40.7 jit_solution(6549706032551895458)
XLA Ops:
  0.0 40.0 %shard_map.55 = bf16[1,32,4096]{2,1,0:T(8,128)(2,1)S(1)} custom-call(bf16[1,32,4096]{2,1,0:T(8,128)(2,1)} %act_hbm.1, f32[1,4096]{1,0:T(1,128)} %gain_hbm.1, s32[1,32]{1,0:T(1,128)} %bitcast.1, bf16[1,4096,5120]{2,1,0:T(8,128)(2,1)} %first_hbm.1, bf16[1,5120,4096]{2,1,0:T(8,128)(2,1)} %second_hbm.1), custom_call_target="tpu_custom_call" | custom-call | tf_op jit(solution)/shard_map/pallas_call | solution.py:234
  40.0 0.7 %copy.7 = bf16[1,32,4096]{2,1,0:T(8,128)(2,1)} copy(bf16[1,32,4096]{2,1,0:T(8,128)(2,1)S(1)} %shard_map.55) | data formatting | bytes 524288
where the time goes:
time: 41.3 us; the launch traced here: 40.7 us
  Pallas kernels  40 us (97%)
  local copies, waits for them, and re-layouts  0.71 us (2%)
    pallas_call x1, Pallas kernels, per_device(): pl.pallas_call(functools.partial(kernel, sections, n, capacity), out_shap...  40 us

commit v1 on v0

v1 whole, which is shorter than its diff:
```python
import functools
import math

import jax
import jax.numpy as jnp
from jax import lax
from jax.experimental import pallas as pl
from jax.experimental.pallas import tpu as pltpu
from jax.sharding import PartitionSpec as P

EXPERTS = 8
SLOTS = 10
EARLY = 4
PARTS = 1
PIECES = 1
STAGES = 8
MESH = pl.DeviceIdType.MESH
F32, BF16 = jnp.float32, jnp.bfloat16

epsilon = 1e-06


def divisor(size, most):
    return max(k for k in range(128, most + 1, 128) if size % k == 0)


def placement(routed, ranks, capacity, groups, count):
    row = lax.broadcasted_iota(jnp.int32, (count * capacity, routed.shape[1]), 0)
    owner = row // (capacity * groups)
    return jnp.where((owner == routed) & (row % capacity == ranks), 1.0, 0.0).astype(F32)


def kernel(
    sections, n, capacity, act_hbm, gain_hbm, ids_hbm, first_hbm, second_hbm, out,
    act, gain, ids, pool, normed, packed, received, total, hidden, outgoing, returned,
    where_to, residual, where_from,
    small_sem, pool_sem, pass_send, pass_recv, send_sem, recv_sem, back_send, back_recv, stage_sem,
):
    section, me = lax.axis_index("section"), lax.axis_index("expert")
    following = lax.rem(section + 1, sections)
    groups = n // EXPERTS
    tokens, width = act.shape
    ff = hidden.shape[1]
    steps, depth = packed.shape[0], packed.shape[3]
    sends, piece_columns = outgoing.shape[0], outgoing.shape[3]
    columns = pool.shape[2]
    slots = pool.shape[0]
    chunks = tiles = width // columns
    loads = chunks + tiles
    block = math.gcd(ff, columns)
    across = columns // block

    def place(j):
        return (j // across) * columns, (j % across) * block

    def load_first(c):
        rows = pl.ds(pl.multiple_of(c * columns, columns), columns)
        for j in range(ff // block):
            top, left = place(j)
            pltpu.make_async_copy(
                first_hbm.at[0, rows, j * block:(j + 1) * block],
                pool.at[c, top:top + columns, left:left + block],
                pool_sem.at[c],
            ).start()

    def wait_first(c):
        rows = first_hbm.at[0, pl.ds(pl.multiple_of(c * columns, columns), columns), :]
        pltpu.make_async_copy(rows, rows, pool_sem.at[c]).wait()

    def second_copy(t):
        cols = pl.ds(pl.multiple_of(t * columns, columns), columns)
        slot = lax.rem(t + chunks, slots)
        return pltpu.make_async_copy(second_hbm.at[0, :, cols], pool.at[slot, 0:ff, :], pool_sem.at[slot])

    def dispatch(c, peer):
        pltpu.make_async_remote_copy(
            src_ref=packed.at[c, peer // groups],
            dst_ref=received.at[c, me],
            send_sem=send_sem.at[c],
            recv_sem=recv_sem.at[c],
            device_id=(section, peer),
            device_id_type=MESH,
        ).start()

    smalls = [
        pltpu.make_async_copy(act_hbm.at[0], act, small_sem.at[0]),
        pltpu.make_async_copy(gain_hbm, gain, small_sem.at[1]),
        pltpu.make_async_copy(ids_hbm, ids, small_sem.at[2]),
    ]
    line = n // 2
    staged = n % 2 == 0 and line <= STAGES
    at = me // 2
    pair = me + 1 - 2 * lax.rem(me, 2)

    def ahead(distance, act_on):
        for base, by in ((me, distance), (pair, distance - 1)):
            if by == 0:
                act_on(base)
            elif by < line:
                @pl.when(at + by < line)
                def _():
                    act_on(base + 2 * by)

                @pl.when(at >= by)
                def _():
                    act_on(base - 2 * by)

    reach = (line + 1) // 2
    near_count = 1
    for by in range(1, reach + 1):
        both = 1 if by == reach else 2
        near_count += both * (jnp.where(at >= by, 1, 0) + jnp.where(at + by < line, 1, 0))

    def near(act_on):
        for distance in range(1, reach + 1):
            ahead(distance, act_on)

    def greet(sem, peer_section, peer):
        pl.semaphore_signal(sem, inc=1, device_id=(peer_section, peer), device_id_type=MESH)

    barrier = pltpu.get_barrier_semaphore()
    previous = lax.rem(section + sections - 1, sections)
    for copy in smalls:
        copy.start()
    if staged:
        near(lambda peer: greet(barrier, section, peer))
        greet(barrier, previous, me)
    else:
        def greet_one(i, carry):
            greet(barrier, section, lax.rem(me + i, n))
            return carry

        def greet_previous(i, carry):
            greet(barrier, previous, i)
            return carry

        lax.fori_loop(1, n, greet_one, 0)
        lax.fori_loop(0, n, greet_previous, 0)

    def start_first(c, carry):
        load_first(c)
        return carry

    def start_second(t, carry):
        second_copy(t).start()
        return carry

    lax.fori_loop(0, chunks, start_first, 0)
    lax.fori_loop(0, slots - chunks, start_second, 0)

    for copy in smalls:
        copy.wait()
    floats = act[...].astype(F32)
    scale = lax.rsqrt(jnp.mean(floats * floats, axis=-1, keepdims=True) + epsilon)
    normed[...] = (floats * scale * gain[...]).astype(BF16)
    routed = ids[...]
    expert = lax.broadcasted_iota(jnp.int32, (EXPERTS, tokens), 0)
    onehot = jnp.where(expert == routed, 1.0, 0.0).astype(F32)
    earlier = lax.broadcasted_iota(jnp.int32, (tokens, tokens), 0) < lax.broadcasted_iota(
        jnp.int32, (tokens, tokens), 1
    )
    before = jnp.dot(
        onehot.astype(BF16), jnp.where(earlier, 1.0, 0.0).astype(BF16), preferred_element_type=F32
    )
    ranks = jnp.sum(before * onehot, axis=0, keepdims=True).astype(jnp.int32)
    placing = placement(routed, ranks, capacity, 1, EXPERTS).astype(BF16)
    for c in range(steps):
        rows = jnp.dot(placing, normed[:, c * depth:(c + 1) * depth], preferred_element_type=F32)
        packed[c] = rows.astype(BF16).reshape(EXPERTS, capacity, depth)
    back = placement(routed, ranks, capacity, groups, where_to.shape[1] // capacity)
    where_to[...] = back.T.astype(BF16)

    def over_steps(low, high, *distances):
        def one(c, carry):
            for distance in distances:
                ahead(distance, lambda peer: dispatch(c, peer))
            return carry

        lax.fori_loop(low, high, one, 0)

    passes = [
        pltpu.make_async_remote_copy(
            src_ref=src, dst_ref=dst, send_sem=pass_send.at[k], recv_sem=pass_recv.at[k],
            device_id=(following, me), device_id_type=MESH,
        )
        for k, (src, dst) in enumerate(((act, residual), (where_to, where_from)))
    ]
    half = n // 2
    if staged:
        early = min(steps, EARLY)
        pl.semaphore_wait(barrier, near_count + 1)
        near(lambda peer: greet(stage_sem, section, peer))
        close, farther = tuple(range(reach, 0, -1)), tuple(range(line, reach, -1))
        over_steps(0, early, *close)
        pl.semaphore_wait(stage_sem, near_count)
        over_steps(0, early, *farther)
        over_steps(early, steps, *farther, *close)
        for copy in passes:
            copy.start()
    else:
        pl.semaphore_wait(barrier, 2 * n - 1)

        def one(c, carry):
            def to_one(i, inner):
                step = (i + 1) // 2
                dispatch(c, lax.rem(me + half + jnp.where(lax.rem(i, 2) == 0, step, n - step), n))
                return inner

            lax.fori_loop(0, n - 1, to_one, 0)
            return carry

        lax.fori_loop(0, steps, one, 0)
        for copy in passes:
            copy.start()

    def keep(c, carry):
        pltpu.make_async_copy(packed.at[c, me // groups], received.at[c, me], recv_sem.at[c]).start()
        return carry

    lax.fori_loop(0, steps, keep, 0)

    parts = steps // chunks

    def multiply(c, kind):
        wait_first(c)
        for p in range(parts):
            step = c * parts + p
            pltpu.make_async_copy(received.at[step], received.at[step], recv_sem.at[step]).wait()
            rows = received[step].reshape(n * capacity, depth)
            for j in range(ff // block):
                top, left = place(j)
                cols = slice(j * block, (j + 1) * block)
                value = jnp.dot(
                    rows, pool[c, top + p * depth:top + (p + 1) * depth, left:left + block],
                    preferred_element_type=F32,
                )
                if kind != "start" or p:
                    value = value + total[:, cols]
                if kind == "end" and p == parts - 1:
                    hidden[:, cols] = jax.nn.gelu(value, approximate=True).astype(BF16)
                else:
                    total[:, cols] = value

    def more(c):
        @pl.when(c + slots < loads)
        def _():
            second_copy(c + slots - chunks).start()

    multiply(0, "start")
    more(0)

    def middle(c, carry):
        multiply(c, "middle")
        more(c)
        return carry

    lax.fori_loop(1, chunks - 1, middle, 0)
    multiply(chunks - 1, "end")
    more(chunks - 1)

    pieces = sends // tiles

    def tile(t, carry):
        second_copy(t).wait()
        slot = lax.rem(t + chunks, slots)
        for j in range(pieces):
            cols = slice(j * piece_columns, (j + 1) * piece_columns)
            piece = jnp.dot(hidden[...], pool[slot, 0:ff, cols], preferred_element_type=F32)
            u = t * pieces + j
            outgoing[u] = piece.astype(BF16).reshape(n, capacity, piece_columns)

            def give(i, inner):
                peer = lax.rem(half * (1 - me // half + i // half) + lax.rem(me + i, half), n)
                pltpu.make_async_remote_copy(
                    src_ref=outgoing.at[u, peer],
                    dst_ref=returned.at[u, me],
                    send_sem=back_send.at[u],
                    recv_sem=back_recv.at[u],
                    device_id=(following, peer),
                    device_id_type=MESH,
                ).start()
                return inner

            lax.fori_loop(0, n, give, 0)
        @pl.when(t + chunks + slots < loads)
        def _():
            second_copy(t + slots).start()

        return carry

    lax.fori_loop(0, tiles, tile, 0)

    for copy in passes:
        copy.wait()
    picks = where_from[:, :n * capacity]

    def combine(u, carry):
        pltpu.make_async_copy(returned.at[u], returned.at[u], back_recv.at[u]).wait()
        cols = pl.ds(pl.multiple_of(u * piece_columns, piece_columns), piece_columns)
        mixed = jnp.dot(picks, returned[u].reshape(n * capacity, piece_columns), preferred_element_type=F32)
        out[0, :, cols] = (residual[:, cols].astype(F32) + mixed).astype(BF16)
        return carry

    lax.fori_loop(0, sends, combine, 0)

    def finish(u, carry):
        pltpu.make_async_copy(outgoing.at[u], outgoing.at[u], back_send.at[u]).wait()
        return carry

    lax.fori_loop(0, sends, finish, 0)

    def drain(c, carry):
        done = received.at[c, pl.ds(0, n - 1)]
        pltpu.make_async_copy(done, done, send_sem.at[c]).wait()
        return carry

    lax.fori_loop(0, steps, drain, 0)


def per_device(sections, n, activations, norm_gain, in_proj, out_proj, expert_ids):
    tokens, width = activations.shape[1:]
    ff = in_proj.shape[2]
    capacity = 2 * tokens // EXPERTS
    columns = divisor(width, 512)
    depth, piece_columns = columns // PARTS, columns // PIECES
    chunks = width // columns
    steps, sends = width // depth, width // piece_columns
    slots = max(chunks, min(SLOTS, 2 * chunks))
    block = math.gcd(ff, columns)
    bands = -(-(ff // block) // (columns // block))
    rows = n * capacity
    lanes = max(128, rows)
    dma = pltpu.SemaphoreType.DMA
    return pl.pallas_call(
        functools.partial(kernel, sections, n, capacity),
        out_shape=pltpu.VMEM(activations.shape, activations.dtype),
        in_specs=[pl.BlockSpec(memory_space=pl.ANY)] * 5,
        out_specs=pl.BlockSpec(memory_space=pltpu.VMEM),
        scratch_shapes=[
            pltpu.VMEM((tokens, width), BF16),
            pltpu.VMEM((1, width), F32),
            pltpu.VMEM((1, tokens), jnp.int32),
            pltpu.VMEM((slots, max(ff, bands * columns), columns), BF16),
            pltpu.VMEM((tokens, width), BF16),
            pltpu.VMEM((steps, EXPERTS, capacity, depth), BF16),
            pltpu.VMEM((steps, n, capacity, depth), BF16),
            pltpu.VMEM((rows, ff), F32),
            pltpu.VMEM((rows, ff), BF16),
            pltpu.VMEM((sends, n, capacity, piece_columns), BF16),
            pltpu.VMEM((sends, n, capacity, piece_columns), BF16),
            pltpu.VMEM((tokens, lanes), BF16),
            pltpu.VMEM((tokens, width), BF16),
            pltpu.VMEM((tokens, lanes), BF16),
            dma((3,)),
            dma((slots,)),
            dma((2,)),
            dma((2,)),
            dma((steps,)),
            dma((steps,)),
            dma((sends,)),
            dma((sends,)),
            pltpu.SemaphoreType.REGULAR,
        ],
        compiler_params=pltpu.CompilerParams(
            collective_id=0, has_side_effects=True, vmem_limit_bytes=62 * 1024 * 1024
        ),
    )(activations, norm_gain, expert_ids.reshape(1, tokens), in_proj, out_proj)


def solution(mesh):
    return jax.shard_map(
        functools.partial(per_device, mesh.shape["section"], mesh.shape["expert"]),
        mesh=mesh,
        in_specs=(
            P("section", "expert", None),
            P("section", None),
            P("section", None, "expert"),
            P("section", "expert", None),
            P("section", "expert", None),
        ),
        out_specs=P("section", "expert", None),
        check_vma=False,
    )
```

time: 41.3 us -> 38.3 us (0.927); the launches traced: 40.7 us -> 38.2 us
  Pallas kernels: 40 us -> 37.5 us
    pallas_call x1, Pallas kernels: 40 us -> 37.5 us  [per_device(): pl.pallas_call(functools.partial(kernel, sections, n, capacity), out_shap...]
where the time goes in v1:
time: 38.3 us; the launch traced here: 38.2 us
  Pallas kernels  37.5 us (98%)
  local copies, waits for them, and re-layouts  0.71 us (2%)
    pallas_call x1, Pallas kernels, per_device(): pl.pallas_call(functools.partial(kernel, sections, n, capacity), out_shap...  37.5 us

profile of v1, /device:TPU:1, one launch (start us, length us, event | category | flops | bytes accessed | tf_op | source)
XLA Modules:
  0.0 38.2 jit_solution(15385779551856513872)
XLA Ops:
  0.0 37.5 %shard_map.55 = bf16[1,32,4096]{2,1,0:T(8,128)(2,1)S(1)} custom-call(bf16[1,32,4096]{2,1,0:T(8,128)(2,1)} %act_hbm.1, f32[1,4096]{1,0:T(1,128)} %gain_hbm.1, s32[1,32]{1,0:T(1,128)} %bitcast.1, bf16[1,4096,5120]{2,1,0:T(8,128)(2,1)} %first_hbm.1, bf16[1,5120,4096]{2,1,0:T(8,128)(2,1)} %second_hbm.1), custom_call_target="tpu_custom_call" | custom-call | tf_op jit(solution)/shard_map/pallas_call | solution.py:334
  37.5 0.7 %copy.7 = bf16[1,32,4096]{2,1,0:T(8,128)(2,1)} copy(bf16[1,32,4096]{2,1,0:T(8,128)(2,1)S(1)} %shard_map.55) | data formatting | bytes 524288

commit v2 on v1

--- a/solution.py
+++ b/solution.py
@@ -10,10 +10,8 @@
 
 EXPERTS = 8
 SLOTS = 10
-EARLY = 4
 PARTS = 1
 PIECES = 1
-STAGES = 8
 MESH = pl.DeviceIdType.MESH
 F32, BF16 = jnp.float32, jnp.bfloat16
 
@@ -34,7 +32,7 @@
     sections, n, capacity, act_hbm, gain_hbm, ids_hbm, first_hbm, second_hbm, out,
     act, gain, ids, pool, normed, packed, received, total, hidden, outgoing, returned,
     where_to, residual, where_from,
-    small_sem, pool_sem, pass_send, pass_recv, send_sem, recv_sem, back_send, back_recv, stage_sem,
+    small_sem, pool_sem, pass_send, pass_recv, send_sem, recv_sem, back_send, back_recv,
 ):
     section, me = lax.axis_index("section"), lax.axis_index("expert")
     following = lax.rem(section + 1, sections)
@@ -87,33 +85,6 @@
         pltpu.make_async_copy(gain_hbm, gain, small_sem.at[1]),
         pltpu.make_async_copy(ids_hbm, ids, small_sem.at[2]),
     ]
-    line = n // 2
-    staged = n % 2 == 0 and line <= STAGES
-    at = me // 2
-    pair = me + 1 - 2 * lax.rem(me, 2)
-
-    def ahead(distance, act_on):
-        for base, by in ((me, distance), (pair, distance - 1)):
-            if by == 0:
-                act_on(base)
-            elif by < line:
-                @pl.when(at + by < line)
-                def _():
-                    act_on(base + 2 * by)
-
-                @pl.when(at >= by)
-                def _():
-                    act_on(base - 2 * by)
-
-    reach = (line + 1) // 2
-    near_count = 1
-    for by in range(1, reach + 1):
-        both = 1 if by == reach else 2
-        near_count += both * (jnp.where(at >= by, 1, 0) + jnp.where(at + by < line, 1, 0))
-
-    def near(act_on):
-        for distance in range(1, reach + 1):
-            ahead(distance, act_on)
 
     def greet(sem, peer_section, peer):
         pl.semaphore_signal(sem, inc=1, device_id=(peer_section, peer), device_id_type=MESH)
@@ -122,20 +93,16 @@
     previous = lax.rem(section + sections - 1, sections)
     for copy in smalls:
         copy.start()
-    if staged:
-        near(lambda peer: greet(barrier, section, peer))
-        greet(barrier, previous, me)
-    else:
-        def greet_one(i, carry):
-            greet(barrier, section, lax.rem(me + i, n))
-            return carry
-
-        def greet_previous(i, carry):
-            greet(barrier, previous, i)
-            return carry
-
-        lax.fori_loop(1, n, greet_one, 0)
-        lax.fori_loop(0, n, greet_previous, 0)
+    def greet_one(i, carry):
+        greet(barrier, section, lax.rem(me + i, n))
+        return carry
+
+    def greet_previous(i, carry):
+        greet(barrier, previous, i)
+        return carry
+
+    lax.fori_loop(1, n, greet_one, 0)
+    lax.fori_loop(0, n, greet_previous, 0)
 
     def start_first(c, carry):
         load_first(c)
@@ -170,14 +137,6 @@
     back = placement(routed, ranks, capacity, groups, where_to.shape[1] // capacity)
     where_to[...] = back.T.astype(BF16)
 
-    def over_steps(low, high, *distances):
-        def one(c, carry):
-            for distance in distances:
-                ahead(distance, lambda peer: dispatch(c, peer))
-            return carry
-
-        lax.fori_loop(low, high, one, 0)
-
     passes = [
         pltpu.make_async_remote_copy(
             src_ref=src, dst_ref=dst, send_sem=pass_send.at[k], recv_sem=pass_recv.at[k],
@@ -186,32 +145,19 @@
         for k, (src, dst) in enumerate(((act, residual), (where_to, where_from)))
     ]
     half = n // 2
-    if staged:
-        early = min(steps, EARLY)
-        pl.semaphore_wait(barrier, near_count + 1)
-        near(lambda peer: greet(stage_sem, section, peer))
-        close, farther = tuple(range(reach, 0, -1)), tuple(range(line, reach, -1))
-        over_steps(0, early, *close)
-        pl.semaphore_wait(stage_sem, near_count)
-        over_steps(0, early, *farther)
-        over_steps(early, steps, *farther, *close)
-        for copy in passes:
-            copy.start()
-    else:
-        pl.semaphore_wait(barrier, 2 * n - 1)
-
-        def one(c, carry):
-            def to_one(i, inner):
-                step = (i + 1) // 2
-                dispatch(c, lax.rem(me + half + jnp.where(lax.rem(i, 2) == 0, step, n - step), n))
-                return inner
-
-            lax.fori_loop(0, n - 1, to_one, 0)
-            return carry
-
-        lax.fori_loop(0, steps, one, 0)
-        for copy in passes:
-            copy.start()
+    pl.semaphore_wait(barrier, 2 * n - 1)
+
+    def one(c, carry):
+        def to_one(i, inner):
+            dispatch(c, lax.rem(half * (1 - me // half + i // half) + lax.rem(me + i + i // half, half), n))
+            return inner
+
+        lax.fori_loop(0, n - 1, to_one, 0)
+        return carry
+
+    lax.fori_loop(0, steps, one, 0)
+    for copy in passes:
+        copy.start()
 
     def keep(c, carry):
         pltpu.make_async_copy(packed.at[c, me // groups], received.at[c, me], recv_sem.at[c]).start()
@@ -255,13 +201,15 @@
         return carry
 
     lax.fori_loop(1, chunks - 1, middle, 0)
+    second_copy(0).wait()
     multiply(chunks - 1, "end")
     more(chunks - 1)
 
     pieces = sends // tiles
 
     def tile(t, carry):
-        second_copy(t).wait()
+        if not isinstance(t, int):
+            second_copy(t).wait()
         slot = lax.rem(t + chunks, slots)
         for j in range(pieces):
             cols = slice(j * piece_columns, (j + 1) * piece_columns)
@@ -288,7 +236,8 @@
 
         return carry
 
-    lax.fori_loop(0, tiles, tile, 0)
+    tile(0, 0)
+    lax.fori_loop(1, tiles, tile, 0)
 
     for copy in passes:
         copy.wait()
@@ -359,7 +308,6 @@
             dma((steps,)),
             dma((sends,)),
             dma((sends,)),
-            pltpu.SemaphoreType.REGULAR,
         ],
         compiler_params=pltpu.CompilerParams(
             collective_id=0, has_side_effects=True, vmem_limit_bytes=62 * 1024 * 1024

time: 38.3 us -> 37.4 us (0.977)
  Pallas kernels: 37.5 us -> 36.4 us
    pallas_call x1, Pallas kernels: 37.5 us -> 36.4 us  [per_device(): pl.pallas_call(functools.partial(kernel, sections, n, capacity), out_shap...]
where the time goes in v2:
time: 37.4 us; the launch traced here: 37.1 us
  Pallas kernels  36.4 us (97%)
  local copies, waits for them, and re-layouts  0.71 us (2%)
    pallas_call x1, Pallas kernels, per_device(): pl.pallas_call(functools.partial(kernel, sections, n, capacity), out_shap...  36.4 us

profile of v2, /device:TPU:1, one launch (start us, length us, event | category | flops | bytes accessed | tf_op | source)
XLA Modules:
  0.0 37.1 jit_solution(6988501827262189696)
XLA Ops:
  0.0 36.4 %shard_map.55 = bf16[1,32,4096]{2,1,0:T(8,128)(2,1)S(1)} custom-call(bf16[1,32,4096]{2,1,0:T(8,128)(2,1)} %act_hbm.1, f32[1,4096]{1,0:T(1,128)} %gain_hbm.1, s32[1,32]{1,0:T(1,128)} %bitcast.1, bf16[1,4096,5120]{2,1,0:T(8,128)(2,1)} %first_hbm.1, bf16[1,5120,4096]{2,1,0:T(8,128)(2,1)} %second_hbm.1), custom_call_target="tpu_custom_call" | custom-call | tf_op jit(solution)/shard_map/pallas_call | solution.py:283
  36.4 0.7 %copy.7 = bf16[1,32,4096]{2,1,0:T(8,128)(2,1)} copy(bf16[1,32,4096]{2,1,0:T(8,128)(2,1)S(1)} %shard_map.55) | data formatting | bytes 524288
